TPU v7x, 256 devices: a whole 4x4x8 slice. The times are simulated.
256 devices in a mesh: layer: 4 (over z_lo, core), feat: 64 (over y, z_hi, x).
Axes of the slice: x: 4, y: 4, z: 8 (z_hi: 4, z_lo: 2; z = z_hi * 2 + z_lo), core: 2. Of those that a mesh axis runs over, the one named last changes fastest.
Arguments:
- activations: bfloat16 [512, 4, 2304], P('feat', 'layer'), may hold values from -6 to 6
- enc_weight: bfloat16 [4, 2304, 65536], P('layer', None, 'feat'), may hold values from -0.0625 to 0.0625
- dec_weight: bfloat16 [4, 65536, 2304], P('layer', 'feat'), may hold values from -0.03125 to 0.03125
- enc_bias: float32 [65536], P('feat'), may hold values from -3 to 3
- threshold: float32 [65536], P('feat'), may hold values from 0.1 to 1
- dec_bias: float32 [4, 2304], P('layer'), may hold values from -3 to 3
- token_mask: int32 [512], replicated, may hold values 0 or 1
Outputs:
- squared_error: float32 [512, 4], P('feat', 'layer')
- latent_grad: float32 [512, 65536], P(None, 'feat')
- input_grad: bfloat16 [512, 4, 2304], P('feat', 'layer')
All inputs are finite; a program needn't handle non-finite values.
Results may differ from a plain program's by a relative error of at most 0.015.
Values may be sent and summed in bfloat16 or wider, within the bound.
A program may use at most 64 MiB of HBM per device.

v0:
```python
import jax
import jax.numpy as jnp
from jax import lax
from jax.sharding import Mesh
from jax.sharding import PartitionSpec as P

FEAT = ("feat_0", "feat_1", "feat_2")
jump_scale = 0.25


def split_up(array, dim, length):
    before, after = (array.shape[:dim], array.shape[dim + 1 :])
    return jnp.moveaxis(array.reshape(*before, length, -1, *after), dim, 0)


def sent_and_summed(array, axis, dim):
    length = lax.axis_size(axis)
    parts = lax.all_to_all(split_up(array, dim, length), axis, 0, 0, tiled=True)
    return jnp.sum(parts, axis=0)


def sum_by_axis(array, axes, dim):
    far, near = axes
    parts = split_up(array, dim, lax.axis_size(far))
    nearer = sent_and_summed(parts, near, dim + 1)
    arrived = lax.all_to_all(nearer, far, split_axis=0, concat_axis=0, tiled=True)
    return arrived.sum(axis=0)


def shards(activations, enc_weight, dec_weight, enc_bias, threshold, dec_bias, token_mask):
    tok_dev = activations.shape[0]
    partial_value = jnp.einsum(
        "tld,ldf->tf",
        lax.all_gather(activations, FEAT, axis=0, tiled=True),
        enc_weight,
        preferred_element_type=jnp.float32,
    )
    preact = lax.psum(partial_value.astype(jnp.bfloat16), "layer").astype(jnp.float32) + enc_bias
    gating = jax.nn.sigmoid((preact - threshold) / jump_scale)
    latent = (preact * gating).astype(jnp.bfloat16)
    gate_slope = gating + preact * gating * (1.0 - gating) / jump_scale
    first_row = lax.axis_index(FEAT) * tok_dev
    rows = latent
    rebuilt = sum_by_axis(
        jnp.einsum("tf,lfd->tld", rows, dec_weight, preferred_element_type=jnp.float32),
        (("feat_0", "feat_1"), "feat_2"),
        0,
    )
    own_mask = lax.dynamic_slice_in_dim(token_mask, first_row, tok_dev, 0).astype(jnp.float32)[
        :, None, None
    ]
    error = own_mask * (rebuilt + dec_bias[None, :, :] - activations.astype(jnp.float32))
    grad_part = jnp.einsum(
        "tld,lfd->tf",
        lax.all_gather(error.astype(jnp.bfloat16), FEAT, axis=0, tiled=True),
        dec_weight,
        preferred_element_type=jnp.float32,
    )
    squared_error = jnp.mean(error * error, axis=-1)
    latent_grad = lax.psum(grad_part.astype(jnp.bfloat16), "layer").astype(jnp.float32)
    preact_grad = (latent_grad * gate_slope).astype(jnp.bfloat16)
    rows = preact_grad
    grad_terms = sum_by_axis(
        jnp.einsum("tf,ldf->tld", rows, enc_weight, preferred_element_type=jnp.float32),
        (("feat_0", "feat_1"), "feat_2"),
        0,
    )
    input_grad = (grad_terms - error).astype(jnp.bfloat16)
    return (squared_error, latent_grad, input_grad)


def solution(mesh):
    finer = Mesh(
        mesh.devices.reshape(mesh.shape["layer"], 4, 4, 4), ("layer", "feat_0", "feat_1", "feat_2")
    )
    return jax.shard_map(
        shards,
        mesh=finer,
        in_specs=(
            P(FEAT, "layer", None),
            P("layer", None, FEAT),
            P("layer", FEAT, None),
            P(FEAT),
            P(FEAT),
            P("layer", None),
            P(),
        ),
        out_specs=(P(FEAT, "layer"), P(None, FEAT), P(FEAT, "layer", None)),
        check_vma=False,
    )
```

profile of v0, /device:TPU:32, one launch (start us, length us, event | category | flops | bytes accessed | tf_op | source)
XLA Modules:
  0.0 498.0 jit_solution(7002110068138016690)
XLA Ops:
  7.2 0.0 all-gather.3.cloned.1.call-start
  7.2 0.7 all-gather.3.cloned.1.call-update
  7.9 0.0 copy-start.2
  7.9 0.0 copy-start.3
  7.9 0.0 all-reduce.3.cloned.1.call-start
  8.0 84.0 %all-gather.3.cloned.1.call-done = bf16[512,1,2304]{2,0,1:T(8,128)(2,1)} async-done(((bf16[8,1,2304]{2,0,1:T(8,128)(2,1)}), bf16[512,1,2304]{2,0,1:T(8,128)(2,1)}) %all-gather.3.cloned.1.call-update) | async-done | bytes 2359312 | tf_op jit(solution)/shard_map/all_gather | solution.py:34
  91.9 6.6 %fusion.10 = bf16[512,1024]{1,0:T(8,128)(2,1)} fusion(bf16[1,2304,1024]{2,1,0:T(8,128)(2,1)} %param.8, bf16[512,1,2304]{2,0,1:T(8,128)(2,1)} %all-gather.3.cloned.1.call-done), kind=kOutput, calls=%fused_computation.15 | convolution fusion | flops 2416443392 | bytes 8126464 | tf_op jit(solution)/shard_map/tld,ldf->tf/dot_general | solution.py:32
  98.6 0.0 all-reduce.3.cloned.1.call-update
  98.6 44.8 %all-reduce.3.cloned.1.call-done = bf16[512,1024]{1,0:T(8,128)(2,1)} async-done(((bf16[512,1024]{1,0:T(8,128)(2,1)}), bf16[512,1024]{1,0:T(8,128)(2,1)}) %all-reduce.3.cloned.1.call-update) | async-done | bytes 1048592 | tf_op jit(solution)/shard_map/psum | solution.py:38
  143.4 0.0 copy-done.2
  143.4 0.0 copy-done.3
  143.4 1.9 fusion.9
  145.3 4.9 convolution_bitcast_fusion.1
  150.2 0.4 copy.10
  150.6 58.9 %all_to_all.20 = f32[4,16,8,1,2304]{4,2,1,3,0:T(8,128)} all-to-all(f32[4,16,8,1,2304]{4,2,1,3,0:T(8,128)S(1)} %copy.10), channel_id=1, replica_groups=mesh['layer'=4,'feat_0'=4,'feat_1'=4,'feat_2'=4] {'feat_2'}, dimensions={0} | all-to-all | bytes 9437184 | tf_op jit(solution)/shard_map/all_to_all | solution.py:18
  209.6 3.7 reduce_sum.53
  213.3 0.0 copy-start.4
  213.3 0.0 copy-start.1
  213.3 9.2 %all-to-all-start.1 = ((f32[16,8,1,2304]{3,1,2,0:T(8,128)}), f32[16,8,1,2304]{3,1,2,0:T(8,128)S(1)}, u32[]{:S(2)}, u32[]{:S(2)}) async-start(f32[16,8,1,2304]{3,1,2,0:T(8,128)} %bitcast.8), calls=%async_computation.1 | async-start | bytes 2359296 | tf_op jit(solution)/shard_map/all_to_all | solution.py:26
  222.5 0.0 all-gather.5.cloned.1.call-start
  222.6 0.0 copy-done.4
  222.6 0.8 dynamic-slice_convert_fusion
  223.4 31.0 %all-to-all-done.1 = f32[16,8,1,2304]{3,1,2,0:T(8,128)S(1)} async-done(((f32[16,8,1,2304]{3,1,2,0:T(8,128)}), f32[16,8,1,2304]{3,1,2,0:T(8,128)S(1)}, u32[]{:S(2)}, u32[]{:S(2)}) %all-to-all-start.1) | async-done | bytes 1179680 | tf_op jit(solution)/shard_map/all_to_all | solution.py:26
  254.4 0.1 reduce_sum.55
  254.5 0.0 copy-done.1
  254.5 0.7 fusion.23
  255.2 0.0 all-gather.5.cloned.1.call-update
  255.2 0.0 copy-start
  255.2 0.2 all-reduce.5.cloned.1.call-start
  255.5 71.8 %all-gather.5.cloned.1.call-done = bf16[512,1,2304]{2,0,1:T(8,128)(2,1)} async-done(((bf16[8,1,2304]{2,0,1:T(8,128)(2,1)}), bf16[512,1,2304]{2,0,1:T(8,128)(2,1)}) %all-gather.5.cloned.1.call-update) | async-done | bytes 2359312 | tf_op jit(solution)/shard_map/all_gather | solution.py:55
  327.3 6.7 %fusion.15 = bf16[512,1024]{1,0:T(8,128)(2,1)} fusion(bf16[1,1024,2304]{2,1,0:T(8,128)(2,1)} %param.9, bf16[512,1,2304]{2,0,1:T(8,128)(2,1)} %all-gather.5.cloned.1.call-done), kind=kOutput, calls=%fused_computation.16 | convolution fusion | flops 2416443392 | bytes 8126464 | tf_op jit(solution)/shard_map/tld,lfd->tf/dot_general | solution.py:53
  333.9 0.0 all-reduce.5.cloned.1.call-update
  333.9 44.7 %all-reduce.5.cloned.1.call-done = bf16[512,1024]{1,0:T(8,128)(2,1)} async-done(((bf16[512,1024]{1,0:T(8,128)(2,1)}), bf16[512,1024]{1,0:T(8,128)(2,1)}) %all-reduce.5.cloned.1.call-update) | async-done | bytes 1048592 | tf_op jit(solution)/shard_map/psum | solution.py:60
  378.7 0.0 copy-done
  378.7 3.6 multiply_convert_fusion
  382.3 5.0 %convolution_bitcast_fusion = f32[4,16,8,1,2304]{4,2,0,1,3:T(8,128)S(1)} fusion(bf16[16,4,8,1024]{3,2,1,0:T(8,128)(2,1)S(1)} %bitcast.65, bf16[1,2304,1024]{2,1,0:T(8,128)(2,1)} %param.8), kind=kOutput, calls=%fused_computation | convolution fusion | flops 2415919104 | bytes 10485760 | tf_op jit(solution)/shard_map/tf,ldf->tld/dot_general | solution.py:64
  387.3 0.4 copy.11
  387.7 58.9 %all_to_all.21 = f32[4,16,8,1,2304]{4,2,1,3,0:T(8,128)} all-to-all(f32[4,16,8,1,2304]{4,2,1,3,0:T(8,128)S(1)} %copy.11), channel_id=1, replica_groups=mesh['layer'=4,'feat_0'=4,'feat_1'=4,'feat_2'=4] {'feat_2'}, dimensions={0} | all-to-all | bytes 9437184 | tf_op jit(solution)/shard_map/all_to_all | solution.py:18
  446.6 2.7 reduce_sum.58
  449.4 40.7 %all_to_all.22 = f32[16,8,1,2304]{3,1,2,0:T(8,128)S(1)} all-to-all(f32[16,8,1,2304]{3,1,2,0:T(8,128)S(1)} %bitcast.64), channel_id=1, replica_groups=mesh['layer'=4,'feat_0'=4,'feat_1'=4,'feat_2'=4] {'feat_0','feat_1'}, dimensions={0} | all-to-all | bytes 2359296 | tf_op jit(solution)/shard_map/all_to_all | solution.py:26
  490.1 0.1 reduce_sum.60
  490.1 0.8 fusion.20
  490.9 0.5 multiply_bitcast_fusion
  (1 shorter events, 0.0 us)
Async XLA Ops:
  7.2 84.8 %all-gather.3.cloned.1.call-start = ((), (), s32[]{:S(2)}) async-start(), calls=%async_computation.4 | async-start | bytes 2396160 | tf_op jit(solution)/shard_map/all_gather | solution.py:34
  7.9 135.5 %copy-start.2 = (f32[1024]{0:T(1024)S(1)}, f32[1024]{0:T(1024)}, u32[]{:S(2)}) copy-start(f32[1024]{0:T(1024)} %param.11) | copy-start | bytes 12292
  7.9 135.5 %copy-start.3 = (f32[1024]{0:T(1024)S(1)}, f32[1024]{0:T(1024)}, u32[]{:S(2)}) copy-start(f32[1024]{0:T(1024)} %param.10) | copy-start | bytes 12292
  7.9 135.4 %all-reduce.3.cloned.1.call-start = ((), (), s32[]{:S(2)}) async-start(), calls=%async_computation.5 | async-start | bytes 2097152 | tf_op jit(solution)/shard_map/psum | solution.py:38
  213.3 9.3 %copy-start.4 = (f32[1,2304]{1,0:T(1,128)S(1)}, f32[1,2304]{1,0:T(1,128)}, u32[]{:S(2)}) copy-start(f32[1,2304]{1,0:T(1,128)} %param.12) | copy-start | bytes 27652
  213.3 41.2 %copy-start.1 = (bf16[8,1,2304]{2,0,1:T(8,128)(2,1)S(1)}, bf16[8,1,2304]{2,0,1:T(8,128)(2,1)}, u32[]{:S(2)}) copy-start(bf16[8,1,2304]{2,0,1:T(8,128)(2,1)} %param.7) | copy-start | bytes 110596
  213.3 41.1 %all-to-all-start.1 = ((f32[16,8,1,2304]{3,1,2,0:T(8,128)}), f32[16,8,1,2304]{3,1,2,0:T(8,128)S(1)}, u32[]{:S(2)}, u32[]{:S(2)}) async-start(f32[16,8,1,2304]{3,1,2,0:T(8,128)} %bitcast.8), calls=%async_computation.1 | async-start | bytes 2359296 | tf_op jit(solution)/shard_map/all_to_all | solution.py:26
  222.5 104.7 %all-gather.5.cloned.1.call-start = ((), (), s32[]{:S(2)}) async-start(), calls=%async_computation.6 | async-start | bytes 2396160 | tf_op jit(solution)/shard_map/all_gather | solution.py:55
  255.2 123.4 %copy-start = (bf16[512,1024]{1,0:T(8,128)(2,1)S(1)}, bf16[512,1024]{1,0:T(8,128)(2,1)}, u32[]{:S(2)}) copy-start(bf16[512,1024]{1,0:T(8,128)(2,1)} %all-reduce.3.cloned.1.call-done) | copy-start | bytes 3145732
  255.2 123.4 %all-reduce.5.cloned.1.call-start = ((), (), s32[]{:S(2)}) async-start(), calls=%async_computation.7 | async-start | bytes 2097152 | tf_op jit(solution)/shard_map/psum | solution.py:60
Sparse Core Ops, SparseCore 0:
  11.2 80.7 all-gather.2
  98.7 44.6 all-reduce.2
  255.3 71.8 all-gather.4
  334.1 44.5 all-reduce.4
where the time goes:
time: 499 us; the launch traced here: 498 us
  waiting for transfers between devices  277 us (56%)
  blocking collectives  159 us (32%)
  matrix products  23.2 us (5%)
  other arithmetic  14.9 us (3%)
  between operations  13.9 us (3%)
  starting transfers between devices  9.54 us (2%)
    all_to_all x2, blocking collectives, sent_and_summed(): parts = lax.all_to_all(split_up(array, dim, length), axis, 0, 0, tiled=True)  118 us
    all_gather x1, waiting for transfers between devices, shards(): lax.all_gather(activations, FEAT, axis=0, tiled=True)  84 us
    all_gather x1, waiting for transfers between devices, shards(): lax.all_gather(error.astype(jnp.bfloat16), FEAT, axis=0, tiled=True)  71.8 us
    psum x1, waiting for transfers between devices, shards(): lax.psum(partial_value.astype(jnp.bfloat16), 'layer').astype(jnp.float32)  44.8 us
    psum x1, waiting for transfers between devices, shards(): lax.psum(grad_part.astype(jnp.bfloat16), 'layer').astype(jnp.float32)  44.7 us
    all_to_all x1, blocking collectives, sum_by_axis(): lax.all_to_all(nearer, far, split_axis=0, concat_axis=0, tiled=True)  40.7 us
    all_to_all x1, waiting for transfers between devices, sum_by_axis(): lax.all_to_all(nearer, far, split_axis=0, concat_axis=0, tiled=True)  31 us
  transfers between devices with their start and end apart: 5, of which 5 were waited for; matrix products, arithmetic and copies ran while one was open for 0% of the time, Pallas kernels for 0%

commit v1 on v0

--- a/solution.py
+++ b/solution.py
@@ -3,9 +3,15 @@
 from jax import lax
 from jax.sharding import Mesh
 from jax.sharding import PartitionSpec as P
+from jax.lax import all_gather
 
 FEAT = ("feat_0", "feat_1", "feat_2")
 jump_scale = 0.25
+
+
+def extend_streams_all(inp, dev_axis):
+    opened = jnp.sum(all_gather(inp, dev_axis), axis=0)
+    return opened
 
 
 def split_up(array, dim, length):
@@ -57,7 +63,7 @@
         preferred_element_type=jnp.float32,
     )
     squared_error = jnp.mean(error * error, axis=-1)
-    latent_grad = lax.psum(grad_part.astype(jnp.bfloat16), "layer").astype(jnp.float32)
+    latent_grad = extend_streams_all(grad_part.astype(jnp.bfloat16), "layer").astype(jnp.float32)
     preact_grad = (latent_grad * gate_slope).astype(jnp.bfloat16)
     rows = preact_grad
     grad_terms = sum_by_axis(

time: 499 us -> 505 us (1.012)
    all_gather x0 -> x1, waiting for transfers between devices: none -> 46.7 us  [extend_streams_all(): opened = jnp.sum(all_gather(inp, dev_axis), axis=0)]
    psum x1 -> x0, waiting for transfers between devices: 44.7 us -> none  [shards(): lax.psum(grad_part.astype(jnp.bfloat16), 'layer').astype(jnp.float32)]
where the time goes in v1:
time: 505 us; the launch traced here: 504 us
  waiting for transfers between devices  279 us (55%)
  blocking collectives  161 us (32%)
  matrix products  23.2 us (5%)
  other arithmetic  17.1 us (3%)
  between operations  13.9 us (3%)
  starting transfers between devices  9.54 us (2%)
    all_to_all x2, blocking collectives, sent_and_summed(): parts = lax.all_to_all(split_up(array, dim, length), axis, 0, 0, tiled=True)  119 us
    all_gather x1, waiting for transfers between devices, shards(): lax.all_gather(activations, FEAT, axis=0, tiled=True)  84 us
    all_gather x1, waiting for transfers between devices, shards(): lax.all_gather(error.astype(jnp.bfloat16), FEAT, axis=0, tiled=True)  71.8 us
    all_gather x1, waiting for transfers between devices, extend_streams_all(): opened = jnp.sum(all_gather(inp, dev_axis), axis=0)  46.7 us
    psum x1, waiting for transfers between devices, shards(): lax.psum(partial_value.astype(jnp.bfloat16), 'layer').astype(jnp.float32)  44.8 us
    all_to_all x1, blocking collectives, sum_by_axis(): lax.all_to_all(nearer, far, split_axis=0, concat_axis=0, tiled=True)  41.9 us
    all_to_all x1, waiting for transfers between devices, sum_by_axis(): lax.all_to_all(nearer, far, split_axis=0, concat_axis=0, tiled=True)  31 us
  transfers between devices with their start and end apart: 5, of which 5 were waited for; matrix products, arithmetic and copies ran while one was open for 0% of the time, Pallas kernels for 0%

profile of v1, /device:TPU:32, one launch (start us, length us, event | category | flops | bytes accessed | tf_op | source)
XLA Modules:
  0.0 504.1 jit_solution(9363197693395794394)
XLA Ops:
  7.2 0.0 all-gather.5.cloned.1.call-start
  7.2 0.7 all-gather.5.cloned.1.call-update
  7.9 0.0 copy-start.2
  7.9 0.0 copy-start.3
  7.9 0.0 all-reduce.2.cloned.1.call-start
  8.0 84.0 %all-gather.5.cloned.1.call-done = bf16[512,1,2304]{2,0,1:T(8,128)(2,1)} async-done(((bf16[8,1,2304]{2,0,1:T(8,128)(2,1)}), bf16[512,1,2304]{2,0,1:T(8,128)(2,1)}) %all-gather.5.cloned.1.call-update) | async-done | bytes 2359312 | tf_op jit(solution)/shard_map/all_gather | solution.py:40
  91.9 6.6 %fusion.10 = bf16[512,1024]{1,0:T(8,128)(2,1)} fusion(bf16[1,2304,1024]{2,1,0:T(8,128)(2,1)} %param.8, bf16[512,1,2304]{2,0,1:T(8,128)(2,1)} %all-gather.5.cloned.1.call-done), kind=kOutput, calls=%fused_computation.15 | convolution fusion | flops 2416443392 | bytes 8126464 | tf_op jit(solution)/shard_map/tld,ldf->tf/dot_general | solution.py:38
  98.6 0.0 all-reduce.2.cloned.1.call-update
  98.6 44.8 %all-reduce.2.cloned.1.call-done = bf16[512,1024]{1,0:T(8,128)(2,1)} async-done(((bf16[512,1024]{1,0:T(8,128)(2,1)}), bf16[512,1024]{1,0:T(8,128)(2,1)}) %all-reduce.2.cloned.1.call-update) | async-done | bytes 1048592 | tf_op jit(solution)/shard_map/psum | solution.py:44
  143.4 0.0 copy-done.2
  143.4 0.0 copy-done.3
  143.4 1.9 fusion.9
  145.3 4.9 convolution_bitcast_fusion.1
  150.2 0.4 copy.10
  150.6 58.9 %all_to_all.20 = f32[4,16,8,1,2304]{4,2,1,3,0:T(8,128)} all-to-all(f32[4,16,8,1,2304]{4,2,1,3,0:T(8,128)S(1)} %copy.10), channel_id=1, replica_groups=mesh['layer'=4,'feat_0'=4,'feat_1'=4,'feat_2'=4] {'feat_2'}, dimensions={0} | all-to-all | bytes 9437184 | tf_op jit(solution)/shard_map/all_to_all | solution.py:24
  209.6 3.7 reduce_sum.65
  213.3 0.0 copy-start.4
  213.3 0.0 copy-start.1
  213.3 9.2 %all-to-all-start.1 = ((f32[16,8,1,2304]{3,1,2,0:T(8,128)}), f32[16,8,1,2304]{3,1,2,0:T(8,128)S(1)}, u32[]{:S(2)}, u32[]{:S(2)}) async-start(f32[16,8,1,2304]{3,1,2,0:T(8,128)} %bitcast.8), calls=%async_computation.1 | async-start | bytes 2359296 | tf_op jit(solution)/shard_map/all_to_all | solution.py:32
  222.5 0.0 all-gather.7.cloned.1.call-start
  222.6 0.0 copy-done.4
  222.6 0.8 dynamic-slice_convert_fusion
  223.4 31.0 %all-to-all-done.1 = f32[16,8,1,2304]{3,1,2,0:T(8,128)S(1)} async-done(((f32[16,8,1,2304]{3,1,2,0:T(8,128)}), f32[16,8,1,2304]{3,1,2,0:T(8,128)S(1)}, u32[]{:S(2)}, u32[]{:S(2)}) %all-to-all-start.1) | async-done | bytes 1179680 | tf_op jit(solution)/shard_map/all_to_all | solution.py:32
  254.4 0.1 reduce_sum.67
  254.5 0.0 copy-done.1
  254.5 0.7 fusion.23
  255.2 0.0 all-gather.7.cloned.1.call-update
  255.2 0.2 all-gather.9.cloned.1.call-start
  255.4 71.8 %all-gather.7.cloned.1.call-done = bf16[512,1,2304]{2,0,1:T(8,128)(2,1)} async-done(((bf16[8,1,2304]{2,0,1:T(8,128)(2,1)}), bf16[512,1,2304]{2,0,1:T(8,128)(2,1)}) %all-gather.7.cloned.1.call-update) | async-done | bytes 2359312 | tf_op jit(solution)/shard_map/all_gather | solution.py:61
  327.3 6.7 %fusion.15 = bf16[512,1024]{1,0:T(8,128)(2,1)} fusion(bf16[1,1024,2304]{2,1,0:T(8,128)(2,1)} %param.9, bf16[512,1,2304]{2,0,1:T(8,128)(2,1)} %all-gather.7.cloned.1.call-done), kind=kOutput, calls=%fused_computation.16 | convolution fusion | flops 2416443392 | bytes 8126464 | tf_op jit(solution)/shard_map/tld,lfd->tf/dot_general | solution.py:59
  333.9 0.0 all-gather.9.cloned.1.call-update
  333.9 46.7 %all-gather.9.cloned.1.call-done = bf16[2048,1024]{1,0:T(8,128)(2,1)} async-done(((bf16[512,1024]{1,0:T(8,128)(2,1)}), bf16[2048,1024]{1,0:T(8,128)(2,1)}) %all-gather.9.cloned.1.call-update) | async-done | bytes 4194320 | tf_op jit(solution)/shard_map/all_gather | solution.py:13
  380.6 0.0 copy-start
  380.6 3.4 reduce_sum.70
  384.0 0.0 copy-done
  384.0 2.4 multiply_convert_fusion
  386.4 5.0 convolution_bitcast_fusion
  391.4 0.4 copy.11
  391.8 59.7 %all_to_all.21 = f32[4,16,8,1,2304]{4,2,1,3,0:T(8,128)} all-to-all(f32[4,16,8,1,2304]{4,2,1,3,0:T(8,128)S(1)} %copy.11), channel_id=1, replica_groups=mesh['layer'=4,'feat_0'=4,'feat_1'=4,'feat_2'=4] {'feat_2'}, dimensions={0} | all-to-all | bytes 9437184 | tf_op jit(solution)/shard_map/all_to_all | solution.py:24
  451.5 2.7 reduce_sum.71
  454.3 41.9 %all_to_all.22 = f32[16,8,1,2304]{3,1,2,0:T(8,128)S(1)} all-to-all(f32[16,8,1,2304]{3,1,2,0:T(8,128)S(1)} %bitcast.65), channel_id=1, replica_groups=mesh['layer'=4,'feat_0'=4,'feat_1'=4,'feat_2'=4] {'feat_0','feat_1'}, dimensions={0} | all-to-all | bytes 2359296 | tf_op jit(solution)/shard_map/all_to_all | solution.py:32
  496.2 0.1 reduce_sum.73
  496.2 0.8 fusion.20
  497.1 0.5 multiply_bitcast_fusion
  (1 shorter events, 0.0 us)
Async XLA Ops:
  7.2 84.8 %all-gather.5.cloned.1.call-start = ((), (), s32[]{:S(2)}) async-start(), calls=%async_computation.4 | async-start | bytes 2396160 | tf_op jit(solution)/shard_map/all_gather | solution.py:40
  7.9 135.5 %copy-start.2 = (f32[1024]{0:T(1024)S(1)}, f32[1024]{0:T(1024)}, u32[]{:S(2)}) copy-start(f32[1024]{0:T(1024)} %param.11) | copy-start | bytes 12292
  7.9 135.5 %copy-start.3 = (f32[1024]{0:T(1024)S(1)}, f32[1024]{0:T(1024)}, u32[]{:S(2)}) copy-start(f32[1024]{0:T(1024)} %param.10) | copy-start | bytes 12292
  7.9 135.4 %all-reduce.2.cloned.1.call-start = ((), (), s32[]{:S(2)}) async-start(), calls=%async_computation.5 | async-start | bytes 2097152 | tf_op jit(solution)/shard_map/psum | solution.py:44
  213.3 9.3 %copy-start.4 = (f32[1,2304]{1,0:T(1,128)S(1)}, f32[1,2304]{1,0:T(1,128)}, u32[]{:S(2)}) copy-start(f32[1,2304]{1,0:T(1,128)} %param.12) | copy-start | bytes 27652
  213.3 41.2 %copy-start.1 = (bf16[8,1,2304]{2,0,1:T(8,128)(2,1)S(1)}, bf16[8,1,2304]{2,0,1:T(8,128)(2,1)}, u32[]{:S(2)}) copy-start(bf16[8,1,2304]{2,0,1:T(8,128)(2,1)} %param.7) | copy-start | bytes 110596
  213.3 41.1 %all-to-all-start.1 = ((f32[16,8,1,2304]{3,1,2,0:T(8,128)}), f32[16,8,1,2304]{3,1,2,0:T(8,128)S(1)}, u32[]{:S(2)}, u32[]{:S(2)}) async-start(f32[16,8,1,2304]{3,1,2,0:T(8,128)} %bitcast.8), calls=%async_computation.1 | async-start | bytes 2359296 | tf_op jit(solution)/shard_map/all_to_all | solution.py:32
  222.5 104.7 %all-gather.7.cloned.1.call-start = ((), (), s32[]{:S(2)}) async-start(), calls=%async_computation.6 | async-start | bytes 2396160 | tf_op jit(solution)/shard_map/all_gather | solution.py:61
  255.2 125.4 %all-gather.9.cloned.1.call-start = ((), (), s32[]{:S(2)}) async-start(), calls=%async_computation.7 | async-start | bytes 5242880 | tf_op jit(solution)/shard_map/all_gather | solution.py:13
  380.6 3.4 copy-start
Sparse Core Ops, SparseCore 0:
  11.2 80.7 all-gather.4
  98.7 44.6 all-reduce.1
  255.3 71.8 all-gather.6
  334.1 46.4 all-gather.8
